TPU v7x, 32 devices: a whole 2x2x4 slice. The times are simulated.
32 devices in a mesh: head: 8 (over y, x, core), seq: 4 (over z).
Axes of the slice: x: 2, y: 2, z: 4, core: 2. Of those that a mesh axis runs over, the one named last changes fastest.
Arguments:
- query_rows: bfloat16 [512, 16384], P('seq', 'head'), may hold values from -512 to 512
- key_rows: bfloat16 [512, 1024], P('seq'), may hold values from -32 to 32
- value_rows: bfloat16 [512, 1024], P('seq'), may hold values from -6 to 6
- positions: int32 [512], P('seq'), may hold values from 0 to 511, as said below
Outputs:
- attended: bfloat16 [512, 16384], P('seq', 'head')
- hessian: float32 [16384, 16384], P('head', 'seq')
Inputs may be any that keep to these rules, and one draw needn't show every extreme that they name: Each aligned block of 4 spans of 128 tokens is one sequence; each span holds 128 consecutive ascending positions starting at a multiple of 128, and the sequence's spans together hold every position 0 to 511 once.
All inputs are finite; a program needn't handle non-finite values.
Results may differ from a plain program's by a relative error of at most 0.0037.
Values may be sent and summed in bfloat16 or wider, within the bound.
A program may use at most 128 MiB of HBM per device.

v0:
```python
import jax
import jax.numpy as jnp
from jax import lax
from jax.sharding import PartitionSpec as P

HEADS = 128
KVH = 8
HD = 128
SPANS = 4


def from_partner(value, axis, stride):
    mask = 2**stride
    pairs = [(source, source ^ mask) for source in range(lax.axis_size(axis))]
    return lax.ppermute(value, axis, pairs)


def spread(x, axis, root):
    mine = lax.axis_index(axis) == root
    return lax.psum(jnp.where(mine, x, jnp.zeros_like(x)), axis)


def attend_block(queries, key_block, value_block, visible, local_heads, local_tokens, score_scale):
    scores = jnp.dot(queries, key_block.T, preferred_element_type=jnp.float32) * score_scale
    scores = scores.reshape(local_heads, local_tokens, key_block.shape[0])
    masked = jnp.where(visible[None], scores, -jnp.inf)
    row_top = jnp.max(masked, axis=2, keepdims=True)
    weights = jnp.exp(masked - row_top)
    weight_sum = jnp.sum(weights, axis=2, keepdims=True)
    mixed = jnp.dot(
        weights.astype(jnp.bfloat16).reshape(local_heads * local_tokens, key_block.shape[0]),
        value_block,
        preferred_element_type=jnp.float32,
    )
    return mixed.reshape(local_heads, local_tokens, HD) / weight_sum


def on_device(query_rows, key_rows, value_rows, positions):
    local_tokens = query_rows.shape[0]
    local_heads = query_rows.shape[1] // HD
    group_size = HEADS // KVH
    score_scale = HD ** (-0.5)
    head_index = lax.axis_index("head")
    span_index = lax.axis_index("seq")
    seq_devices = lax.axis_size("seq")
    head_devices = lax.axis_size("head")
    key_head = head_index * local_heads // group_size
    key_slice = lax.dynamic_slice_in_dim(key_rows, key_head * HD, HD, 1)
    value_slice = lax.dynamic_slice_in_dim(value_rows, key_head * HD, HD, 1)
    queries = jnp.transpose(query_rows.reshape(local_tokens, local_heads, HD), (1, 0, 2))
    queries = queries.reshape(local_heads * local_tokens, HD)
    key_block, value_block, place_block = (key_slice, value_slice, positions)
    for bit in range(SPANS.bit_length() - 1):
        other_keys, other_values, other_places = from_partner(
            (key_block, value_block, place_block), "seq", bit
        )
        key_block = jnp.concatenate([key_block, other_keys], axis=0)
        value_block = jnp.concatenate([value_block, other_values], axis=0)
        place_block = jnp.concatenate([place_block, other_places], axis=0)
    visible = place_block[None, :] <= positions[:, None]
    outcome = attend_block(
        queries, key_block, value_block, visible, local_heads, local_tokens, score_scale
    )
    attended = (
        jnp.transpose(outcome, (1, 0, 2))
        .reshape(local_tokens, local_heads * HD)
        .astype(jnp.bfloat16)
    )
    row_operand = lax.all_gather(attended, "seq", axis=0, tiled=True)
    root_count = head_devices // seq_devices
    column_parts = []
    for offset in range(root_count):
        column_parts.append(spread(row_operand, "head", span_index * root_count + offset))
    columns = jnp.concatenate(column_parts, axis=1)
    hessian = lax.dot_general(
        row_operand, columns, (((0,), (0,)), ((), ())), preferred_element_type=jnp.float32
    )
    return (attended, hessian)


def solution(mesh):
    placed = (P("seq", "head"), P("seq", None), P("seq", None), P("seq"))
    return jax.shard_map(
        on_device,
        mesh=mesh,
        in_specs=placed,
        out_specs=(P("seq", "head"), P("head", "seq")),
        check_vma=False,
    )
```

profile of v0, /device:TPU:0, one launch (start us, length us, event | category | flops | bytes accessed | tf_op | source)
XLA Modules:
  0.0 186.5 jit_solution(7501032044831482604)
XLA Ops:
  7.2 0.0 copy-start
  7.2 0.0 copy-start.3
  7.2 0.0 all-gather.2.cloned.1.call-start
  7.2 3.1 %collective-permute-start = (s32[128]{0:T(128)}, s32[128]{0:T(128)S(1)}, u32[]{:S(2)}, u32[]{:S(2)}) collective-permute-start(s32[128]{0:T(128)} %param.7), channel_id=1, source_target_pairs={{0,1},{1,0},{2,3},{3,2},{4,5},{5,4},{6,7},{7,6},{8,9},{9,8},{10,11... | collective-permute-start | bytes 1544 | tf_op jit(solution)/shard_map/ppermute | solution.py:15
  10.4 0.0 copy-done
  10.4 0.1 copy.18
  10.5 0.9 collective-permute-start.4
  11.4 0.7 collective-permute-done
  12.0 0.7 pad_add_fusion.1
  12.7 3.0 %collective-permute-start.1 = (s32[256]{0:T(256)S(1)}, s32[256]{0:T(256)S(1)}, u32[]{:S(2)}, u32[]{:S(2)}) collective-permute-start(s32[256]{0:T(256)S(1)} %pad_add_fusion.1), channel_id=1, source_target_pairs={{0,2},{1,3},{2,0},{3,1},{4,6},{5,7},{6,4},{7,5},{8,10},{9,11},{10,... | collective-permute-start | bytes 3080 | tf_op jit(solution)/shard_map/ppermute | solution.py:15
  15.7 0.8 constant_dynamic-slice_fusion.1
  16.5 1.6 collective-permute-start.2
  18.1 1.3 copy.12
  19.4 0.3 copy.13
  19.7 0.0 collective-permute-done.1
  19.7 0.0 copy-done.3
  19.7 0.1 broadcast_compare_fusion
  19.9 0.6 collective-permute-done.2
  20.4 0.1 collective-permute-start.3
  20.5 0.0 collective-permute-done.4
  20.5 2.9 %collective-permute-start.5 = (bf16[256,128]{0,1:T(8,128)(2,1)S(1)}, bf16[256,128]{0,1:T(8,128)(2,1)S(1)}, u32[]{:S(2)}, u32[]{:S(2)}) collective-permute-start(bf16[256,128]{0,1:T(8,128)(2,1)S(1)} %pad_maximum_fusion.1), channel_id=1, source_target_pairs={{0,2},{1,3},{2,0},{3,1},{4,6},{5,7},{6,4},{7,5},{8,10},{9,11},{10,... | collective-permute-start | bytes 196616 | tf_op jit(solution)/shard_map/ppermute | solution.py:15
  23.4 2.2 %collective-permute-done.3 = bf16[256,128]{1,0:T(8,128)(2,1)S(1)} collective-permute-done((bf16[256,128]{1,0:T(8,128)(2,1)S(1)}, bf16[256,128]{1,0:T(8,128)(2,1)S(1)}, u32[]{:S(2)}, u32[]{:S(2)}) %collective-permute-start.3) | collective-permute-done | bytes 65568 | tf_op jit(solution)/shard_map/ppermute | solution.py:15
  25.6 0.3 broadcast_in_dim.19
  25.9 1.0 fusion.20
  26.8 0.7 fusion.4
  27.5 2.5 %copy.17 = bf16[2048,512]{1,0:T(8,128)(2,1)} copy(bf16[2048,512]{0,1:T(8,128)(2,1)S(1)} %get-tuple-element.11) | data formatting | bytes 4194304 | tf_op jit(solution)/shard_map/dot_general | solution.py:30
  30.0 0.0 collective-permute-done.5
  30.0 3.2 %fusion.7 = bf16[128,16,128]{0,2,1:T(8,128)(2,1)} fusion(bf16[16,128,512]{2,1,0:T(8,128)(2,1)} %bitcast.28, f32[128,16]{0,1:T(8,128)S(1)} %bitcast.34, bf16[256,128]{0,1:T(8,128)(2,1)S(1)} %collective-permute-done.5, bf16[128,128]{0,1:T(8,128)(2,1)S(1)} %collective-permute-done.4, bf16[128,128]{0,1:T(8,128)(2,1)S(1)} %copy.18), kind=kOutput, calls=%fused_computation.12 | convolution fusion | flops 269352960 | bytes 2760704 | tf_op jit(solution)/shard_map/dot_general | solution.py:30
  33.2 0.0 all-gather.2.cloned.1.call-update
  33.2 0.0 all-reduce.3.cloned.1.call-start
  33.3 46.2 %all-gather.2.cloned.1.call-done = bf16[512,2048]{0,1:T(8,128)(2,1)} async-done(((bf16[128,2048]{0,1:T(8,128)(2,1)}), bf16[512,2048]{0,1:T(8,128)(2,1)}) %all-gather.2.cloned.1.call-update) | async-done | bytes 2097168 | tf_op jit(solution)/shard_map/all_gather | solution.py:69
  79.5 3.9 %broadcast_select_fusion.1 = (bf16[512,2048]{0,1:T(8,128)(2,1)}, bf16[512,2048]{0,1:T(8,128)(2,1)}) fusion(bf16[512,2048]{0,1:T(8,128)(2,1)} %all-gather.2.cloned.1.call-done, pred[]{:T(512)S(6)} %eq.6, pred[]{:T(512)S(6)} %eq.7), kind=kLoop, calls=%fused_computation.9 | loop fusion | flops 2097152 | bytes 6291458 | tf_op jit(solution)/shard_map/jit(_where)/select_n | solution.py:20
  83.4 0.0 copy-start.2
  83.4 0.0 copy-start.1
  83.4 0.0 all-reduce.3.cloned.1.call-update
  83.4 1.0 copy-done.2
  84.4 1.0 copy.16
  85.4 77.2 %all-reduce.3.cloned.1.call-done = (bf16[512,2048]{0,1:T(8,128)(2,1)}, bf16[512,2048]{0,1:T(8,128)(2,1)}) async-done(((bf16[512,2048]{0,1:T(8,128)(2,1)}, bf16[512,2048]{0,1:T(8,128)(2,1)}), (bf16[512,2048]{0,1:T(8,128)(2,1)}, bf16[512,2048]{0,1:T(8,128)(2,1)})) %all-reduce.3.cloned.1.call-update) | async-done | bytes 4194320 | tf_op jit(solution)/shard_map/psum | solution.py:20
  162.6 0.0 copy-done.1
  162.6 17.1 %fusion = f32[2048,4096]{1,0:T(8,128)} fusion(bf16[512,2048]{0,1:T(8,128)(2,1)S(1)} %copy-done.1, bf16[512,2048]{0,1:T(8,128)(2,1)} %get-tuple-element.8, bf16[512,2048]{0,1:T(8,128)(2,1)} %get-tuple-element.9), kind=kOutput, calls=%fused_computation | convolution fusion | flops 8598323200 | bytes 39845888 | tf_op jit(solution)/shard_map/dot_general | solution.py:75
  (4 shorter events, 0.0 us)
Async XLA Ops:
  7.2 3.2 %copy-start = (bf16[128,1024]{1,0:T(8,128)(2,1)S(1)}, bf16[128,1024]{1,0:T(8,128)(2,1)}, u32[]{:S(2)}) copy-start(bf16[128,1024]{1,0:T(8,128)(2,1)} %param.6) | copy-start | bytes 786436
  7.2 12.5 %copy-start.3 = (s32[128]{0:T(128)S(1)}, s32[128]{0:T(128)}, u32[]{:S(2)}) copy-start(s32[128]{0:T(128)} %param.7) | copy-start | bytes 1540
  7.2 72.3 %all-gather.2.cloned.1.call-start = ((), (), s32[]{:S(2)}) async-start(), calls=%async_computation | async-start | bytes 2621440 | tf_op jit(solution)/shard_map/all_gather | solution.py:69
  7.2 4.8 %collective-permute-start = (s32[128]{0:T(128)}, s32[128]{0:T(128)S(1)}, u32[]{:S(2)}, u32[]{:S(2)}) collective-permute-start(s32[128]{0:T(128)} %param.7), channel_id=1, source_target_pairs={{0,1},{1,0},{2,3},{3,2},{4,5},{5,4},{6,7},{7,6},{8,9},{9,8},{10,11... | collective-permute-start | bytes 1544 | tf_op jit(solution)/shard_map/ppermute | solution.py:15
  10.5 10.0 %collective-permute-start.4 = (bf16[128,128]{0,1:T(8,128)(2,1)S(1)}, bf16[128,128]{0,1:T(8,128)(2,1)S(1)}, u32[]{:S(2)}, u32[]{:S(2)}) collective-permute-start(bf16[128,128]{0,1:T(8,128)(2,1)S(1)} %copy.18), channel_id=1, source_target_pairs={{0,1},{1,0},{2,3},{3,2},{4,5},{5,4},{6,7},{7,6},{8,9},{9,8},{10,11... | collective-permute-start | bytes 98312 | tf_op jit(solution)/shard_map/ppermute | solution.py:15
  12.7 7.0 %collective-permute-start.1 = (s32[256]{0:T(256)S(1)}, s32[256]{0:T(256)S(1)}, u32[]{:S(2)}, u32[]{:S(2)}) collective-permute-start(s32[256]{0:T(256)S(1)} %pad_add_fusion.1), channel_id=1, source_target_pairs={{0,2},{1,3},{2,0},{3,1},{4,6},{5,7},{6,4},{7,5},{8,10},{9,11},{10,... | collective-permute-start | bytes 3080 | tf_op jit(solution)/shard_map/ppermute | solution.py:15
  16.5 3.9 %collective-permute-start.2 = (bf16[128,128]{1,0:T(8,128)(2,1)S(1)}, bf16[128,128]{1,0:T(8,128)(2,1)S(1)}, u32[]{:S(2)}, u32[]{:S(2)}) collective-permute-start(bf16[128,128]{1,0:T(8,128)(2,1)S(1)} %constant_dynamic-slice_fusion.1), channel_id=1, source_target_pairs={{0,1},{1,0},{2,3},{3,2},{4,5},{5,4},{6,7},{7,6},{8,9},{9,8},{10,11... | collective-permute-start | bytes 98312 | tf_op jit(solution)/shard_map/ppermute | solution.py:15
  20.4 5.2 %collective-permute-start.3 = (bf16[256,128]{1,0:T(8,128)(2,1)S(1)}, bf16[256,128]{1,0:T(8,128)(2,1)S(1)}, u32[]{:S(2)}, u32[]{:S(2)}) collective-permute-start(bf16[256,128]{1,0:T(8,128)(2,1)S(1)} %pad_maximum_fusion), channel_id=1, source_target_pairs={{0,2},{1,3},{2,0},{3,1},{4,6},{5,7},{6,4},{7,5},{8,10},{9,11},{10,... | collective-permute-start | bytes 196616 | tf_op jit(solution)/shard_map/ppermute | solution.py:15
  20.5 9.5 %collective-permute-start.5 = (bf16[256,128]{0,1:T(8,128)(2,1)S(1)}, bf16[256,128]{0,1:T(8,128)(2,1)S(1)}, u32[]{:S(2)}, u32[]{:S(2)}) collective-permute-start(bf16[256,128]{0,1:T(8,128)(2,1)S(1)} %pad_maximum_fusion.1), channel_id=1, source_target_pairs={{0,2},{1,3},{2,0},{3,1},{4,6},{5,7},{6,4},{7,5},{8,10},{9,11},{10,... | collective-permute-start | bytes 196616 | tf_op jit(solution)/shard_map/ppermute | solution.py:15
  33.2 129.4 %all-reduce.3.cloned.1.call-start = ((), (), s32[]{:S(2)}) async-start(), calls=%async_computation.1 | async-start | bytes 8388608 | tf_op jit(solution)/shard_map/psum | solution.py:20
  83.4 1.0 copy-start.2
  83.4 79.2 %copy-start.1 = (bf16[512,2048]{0,1:T(8,128)(2,1)S(1)}, bf16[512,2048]{0,1:T(8,128)(2,1)}, u32[]{:S(2)}) copy-start(bf16[512,2048]{0,1:T(8,128)(2,1)} %all-gather.2.cloned.1.call-done) | copy-start | bytes 6291460
Sparse Core Ops, SparseCore 0:
  33.3 46.0 all-gather.1
  83.5 79.0 all-reduce.2
where the time goes:
time: 187 us; the launch traced here: 186 us
  waiting for transfers between devices  127 us (68%)
  matrix products  21.2 us (11%)
  between operations  14.1 us (8%)
  starting transfers between devices  11.7 us (6%)
  local copies, waits for them, and re-layouts  7.29 us (4%)
  other arithmetic  5.39 us (3%)
    psum x1, waiting for transfers between devices, spread(): return lax.psum(jnp.where(mine, x, jnp.zeros_like(x)), axis)  77.2 us
    all_gather x1, waiting for transfers between devices, on_device(): row_operand = lax.all_gather(attended, 'seq', axis=0, tiled=True)  46.2 us
    dot_general x1, matrix products, on_device(): lax.dot_general(row_operand, columns, (((0,), (0,)), ((), ())), preferred...  17.1 us
    ppermute x6, starting transfers between devices, from_partner(): return lax.ppermute(value, axis, pairs)  11.6 us
    select_n x1, other arithmetic, spread(): return lax.psum(jnp.where(mine, x, jnp.zeros_like(x)), axis)  3.89 us
  transfers between devices with their start and end apart: 8, of which 5 were waited for; matrix products, arithmetic and copies ran while one was open for 5% of the time, Pallas kernels for 0%

commit v1 on v0

--- a/solution.py
+++ b/solution.py
@@ -17,7 +17,7 @@
 
 def spread(x, axis, root):
     mine = lax.axis_index(axis) == root
-    return lax.psum(jnp.where(mine, x, jnp.zeros_like(x)), axis)
+    return jnp.sum(lax.all_gather(jnp.where(mine, x, jnp.zeros_like(x)), axis), axis=0)
 
 
 def attend_block(queries, key_block, value_block, visible, local_heads, local_tokens, score_scale):

time: 187 us -> 331 us (1.77)
  waiting for transfers between devices: 127 us -> 217 us
  local copies, waits for them, and re-layouts: 7.29 us -> 41.9 us
  other arithmetic: 5.39 us -> 26.8 us
    all_gather x0 -> x2, waiting for transfers between devices: none -> 167 us  [spread(): lax.all_gather(jnp.where(mine, x, jnp.zeros_like(x)), axis)]
    psum x1 -> x0, waiting for transfers between devices: 77.2 us -> none  [spread(): return lax.psum(jnp.where(mine, x, jnp.zeros_like(x)), axis)]
    unnamed x11 -> x15, local copies, waits for them, and re-layouts: 3.46 us -> 38.1 us
    reduce_sum x0 -> x1, other arithmetic: none -> 20 us  [spread(): jnp.sum(lax.all_gather(jnp.where(mine, x, jnp.zeros_like(x)), axis), axis=0)]
  transfers between devices with their start and end apart: 8 -> 9, of which waited for: 5 -> 5; matrix products, arithmetic and copies ran while one was open for 5% -> 8% of each run, Pallas kernels for 0% -> 0%
where the time goes in v1:
time: 331 us; the launch traced here: 330 us
  waiting for transfers between devices  217 us (66%)
  local copies, waits for them, and re-layouts  41.9 us (13%)
  other arithmetic  26.8 us (8%)
  matrix products  19 us (6%)
  between operations  13.9 us (4%)
  starting transfers between devices  12 us (4%)
    all_gather x2, waiting for transfers between devices, spread(): lax.all_gather(jnp.where(mine, x, jnp.zeros_like(x)), axis)  167 us
    all_gather x1, waiting for transfers between devices, on_device(): row_operand = lax.all_gather(attended, 'seq', axis=0, tiled=True)  45.5 us
    unnamed x15, local copies, waits for them, and re-layouts  38.1 us
    reduce_sum x1, other arithmetic, spread(): jnp.sum(lax.all_gather(jnp.where(mine, x, jnp.zeros_like(x)), axis), axis=0)  20 us
    dot_general x1, matrix products, on_device(): lax.dot_general(row_operand, columns, (((0,), (0,)), ((), ())), preferred...  14.9 us
    ppermute x6, starting transfers between devices, from_partner(): return lax.ppermute(value, axis, pairs)  11.7 us
  transfers between devices with their start and end apart: 9, of which 5 were waited for; matrix products, arithmetic and copies ran while one was open for 8% of the time, Pallas kernels for 0%

profile of v1, /device:TPU:0, one launch (start us, length us, event | category | flops | bytes accessed | tf_op | source)
XLA Modules:
  0.0 330.4 jit_solution(494997660993604652)
XLA Ops:
  7.2 0.0 copy-start
  7.2 0.0 all-gather.6.cloned.1.call-start
  7.2 3.1 collective-permute-start
  10.3 0.0 copy-done
  10.4 0.1 copy.23
  10.5 0.9 collective-permute-start.4
  11.4 0.7 collective-permute-done
  12.0 0.7 pad_add_fusion.1
  12.7 3.0 collective-permute-start.1
  15.7 0.8 constant_dynamic-slice_fusion.1
  16.5 1.6 collective-permute-start.2
  18.1 1.3 copy.17
  19.4 0.3 copy.18
  19.7 0.0 collective-permute-done.1
  19.7 0.7 pad_add_fusion
  20.3 0.8 broadcast_compare_fusion
  21.1 0.0 collective-permute-done.2
  21.2 0.6 collective-permute-start.3
  21.8 0.0 collective-permute-done.4
  21.8 2.5 collective-permute-start.5
  24.2 2.9 collective-permute-done.3
  27.1 0.3 broadcast_in_dim.19
  27.4 1.0 fusion.20
  28.3 0.7 fusion.4
  29.0 2.5 copy.22
  31.5 0.0 collective-permute-done.5
  31.5 3.2 fusion.7
  34.7 0.0 all-gather.6.cloned.1.call-update
  34.7 0.0 all-gather.8.cloned.1.call-start
  34.8 0.0 copy-start.4
  34.8 45.5 %all-gather.6.cloned.1.call-done = bf16[512,2048]{0,1:T(8,128)(2,1)} async-done(((bf16[128,2048]{0,1:T(8,128)(2,1)}), bf16[512,2048]{0,1:T(8,128)(2,1)}) %all-gather.6.cloned.1.call-update) | async-done | bytes 2097168 | tf_op jit(solution)/shard_map/all_gather | solution.py:69
  80.3 3.9 %broadcast_select_fusion.1 = (bf16[512,2048]{0,1:T(8,128)(2,1)}, bf16[512,2048]{0,1:T(8,128)(2,1)}) fusion(bf16[512,2048]{0,1:T(8,128)(2,1)} %all-gather.6.cloned.1.call-done, pred[]{:T(512)S(6)} %eq.6, pred[]{:T(512)S(6)} %eq.7), kind=kLoop, calls=%fused_computation.11 | loop fusion | flops 2097152 | bytes 6291458 | tf_op jit(solution)/shard_map/jit(_where)/select_n | solution.py:20
  84.2 0.0 all-gather.8.cloned.1.call-update
  84.3 0.2 all-gather.10.cloned.1.call-start
  84.5 0.5 all-gather.10.cloned.1.call-update
  85.0 0.0 copy-done.4
  85.0 1.0 copy.21
  86.0 89.6 %all-gather.8.cloned.1.call-done = bf16[4096,2048]{0,1:T(8,128)(2,1)} async-done(((bf16[512,2048]{0,1:T(8,128)(2,1)}), bf16[4096,2048]{0,1:T(8,128)(2,1)}) %all-gather.8.cloned.1.call-update) | async-done | bytes 16777232 | tf_op jit(solution)/shard_map/all_gather | solution.py:20
  175.6 17.2 %copy.25 = bf16[256,8,8,512]{3,2,1,0:T(8,128)(2,1)} copy(bf16[256,8,8,512]{3,1,2,0:T(8,128)(2,1)} %bitcast.38) | data formatting | bytes 33554432
  192.8 77.7 %all-gather.10.cloned.1.call-done = bf16[4096,2048]{0,1:T(8,128)(2,1)} async-done(((bf16[512,2048]{0,1:T(8,128)(2,1)}), bf16[4096,2048]{0,1:T(8,128)(2,1)}) %all-gather.10.cloned.1.call-update) | async-done | bytes 16777232 | tf_op jit(solution)/shard_map/all_gather | solution.py:20
  270.6 0.0 copy-start.2
  270.6 18.4 %copy.26 = bf16[256,8,8,512]{3,2,1,0:T(8,128)(2,1)} copy(bf16[256,8,8,512]{3,1,2,0:T(8,128)(2,1)} %bitcast.39) | data formatting | bytes 33554432
  289.0 0.0 copy-done.2
  289.0 20.0 %bitcast_reduce_fusion = (bf16[512,2048]{0,1:T(8,128)(2,1)S(1)}, bf16[512,2048]{0,1:T(8,128)(2,1)S(1)}) fusion(bf16[256,8,8,512]{3,2,1,0:T(8,128)(2,1)} %copy.26, bf16[256,8,8,512]{3,2,1,0:T(8,128)(2,1)S(1)} %copy-done.2), kind=kLoop, calls=%fused_computation | loop fusion | flops 14680064 | bytes 37748736 | tf_op jit(solution)/shard_map/reduce_sum | solution.py:20
  309.0 0.0 copy-done.3
  309.0 0.0 copy-start.1
  309.0 14.9 %fusion = f32[2048,4096]{1,0:T(8,128)} fusion(bf16[512,2048]{0,1:T(8,128)(2,1)S(1)} %copy-done.3, bf16[512,2048]{0,1:T(8,128)(2,1)S(1)} %get-tuple-element.16, bf16[512,2048]{0,1:T(8,128)(2,1)S(1)} %get-tuple-element.17), kind=kOutput, calls=%fused_computation.2 | convolution fusion | flops 8598323200 | bytes 39845888 | tf_op jit(solution)/shard_map/dot_general | solution.py:75
  323.9 0.0 copy-done.1
  (4 shorter events, 0.0 us)
Async XLA Ops:
  7.2 3.2 copy-start
  7.2 73.1 %all-gather.6.cloned.1.call-start = ((), (), s32[]{:S(2)}) async-start(), calls=%async_computation | async-start | bytes 2621440 | tf_op jit(solution)/shard_map/all_gather | solution.py:69
  7.2 4.8 %collective-permute-start = (s32[128]{0:T(128)}, s32[128]{0:T(128)S(1)}, u32[]{:S(2)}, u32[]{:S(2)}) collective-permute-start(s32[128]{0:T(128)} %param.7), channel_id=1, source_target_pairs={{0,1},{1,0},{2,3},{3,2},{4,5},{5,4},{6,7},{7,6},{8,9},{9,8},{10,11... | collective-permute-start | bytes 1544 | tf_op jit(solution)/shard_map/ppermute | solution.py:15
  10.5 11.3 %collective-permute-start.4 = (bf16[128,128]{0,1:T(8,128)(2,1)S(1)}, bf16[128,128]{0,1:T(8,128)(2,1)S(1)}, u32[]{:S(2)}, u32[]{:S(2)}) collective-permute-start(bf16[128,128]{0,1:T(8,128)(2,1)S(1)} %copy.23), channel_id=1, source_target_pairs={{0,1},{1,0},{2,3},{3,2},{4,5},{5,4},{6,7},{7,6},{8,9},{9,8},{10,11... | collective-permute-start | bytes 98312 | tf_op jit(solution)/shard_map/ppermute | solution.py:15
  12.7 7.0 %collective-permute-start.1 = (s32[256]{0:T(256)S(1)}, s32[256]{0:T(256)S(1)}, u32[]{:S(2)}, u32[]{:S(2)}) collective-permute-start(s32[256]{0:T(256)S(1)} %pad_add_fusion.1), channel_id=1, source_target_pairs={{0,2},{1,3},{2,0},{3,1},{4,6},{5,7},{6,4},{7,5},{8,10},{9,11},{10,... | collective-permute-start | bytes 3080 | tf_op jit(solution)/shard_map/ppermute | solution.py:15
  16.5 4.7 %collective-permute-start.2 = (bf16[128,128]{1,0:T(8,128)(2,1)S(1)}, bf16[128,128]{1,0:T(8,128)(2,1)S(1)}, u32[]{:S(2)}, u32[]{:S(2)}) collective-permute-start(bf16[128,128]{1,0:T(8,128)(2,1)S(1)} %constant_dynamic-slice_fusion.1), channel_id=1, source_target_pairs={{0,1},{1,0},{2,3},{3,2},{4,5},{5,4},{6,7},{7,6},{8,9},{9,8},{10,11... | collective-permute-start | bytes 98312 | tf_op jit(solution)/shard_map/ppermute | solution.py:15
  21.2 5.9 %collective-permute-start.3 = (bf16[256,128]{1,0:T(8,128)(2,1)S(1)}, bf16[256,128]{1,0:T(8,128)(2,1)S(1)}, u32[]{:S(2)}, u32[]{:S(2)}) collective-permute-start(bf16[256,128]{1,0:T(8,128)(2,1)S(1)} %pad_maximum_fusion), channel_id=1, source_target_pairs={{0,2},{1,3},{2,0},{3,1},{4,6},{5,7},{6,4},{7,5},{8,10},{9,11},{10,... | collective-permute-start | bytes 196616 | tf_op jit(solution)/shard_map/ppermute | solution.py:15
  21.8 9.7 %collective-permute-start.5 = (bf16[256,128]{0,1:T(8,128)(2,1)S(1)}, bf16[256,128]{0,1:T(8,128)(2,1)S(1)}, u32[]{:S(2)}, u32[]{:S(2)}) collective-permute-start(bf16[256,128]{0,1:T(8,128)(2,1)S(1)} %pad_maximum_fusion.1), channel_id=1, source_target_pairs={{0,2},{1,3},{2,0},{3,1},{4,6},{5,7},{6,4},{7,5},{8,10},{9,11},{10,... | collective-permute-start | bytes 196616 | tf_op jit(solution)/shard_map/ppermute | solution.py:15
  34.7 140.9 %all-gather.8.cloned.1.call-start = ((), (), s32[]{:S(2)}) async-start(), calls=%async_computation.1 | async-start | bytes 18874368 | tf_op jit(solution)/shard_map/all_gather | solution.py:20
  34.8 50.2 %copy-start.4 = (bf16[128,16,128]{0,2,1:T(8,128)(2,1)S(1)}, bf16[128,16,128]{0,2,1:T(8,128)(2,1)}, u32[]{:S(2)}) copy-start(bf16[128,16,128]{0,2,1:T(8,128)(2,1)} %fusion.7) | copy-start | bytes 1572868
  84.3 186.3 %all-gather.10.cloned.1.call-start = ((), (), s32[]{:S(2)}) async-start(), calls=%async_computation.2 | async-start | bytes 18874368 | tf_op jit(solution)/shard_map/all_gather | solution.py:20
  270.6 18.4 %copy-start.2 = (bf16[256,8,8,512]{3,2,1,0:T(8,128)(2,1)S(1)}, bf16[256,8,8,512]{3,2,1,0:T(8,128)(2,1)}, u32[]{:S(2)}) copy-start(bf16[256,8,8,512]{3,2,1,0:T(8,128)(2,1)} %copy.25) | copy-start | bytes 50331652
  289.0 20.1 %copy-start.3 = (bf16[512,2048]{0,1:T(8,128)(2,1)S(1)}, bf16[512,2048]{0,1:T(8,128)(2,1)}, u32[]{:S(2)}) copy-start(bf16[512,2048]{0,1:T(8,128)(2,1)} %all-gather.6.cloned.1.call-done) | copy-start | bytes 6291460
  309.0 14.9 %copy-start.1 = (bf16[128,1024]{1,0:T(8,128)(2,1)S(1)}, bf16[128,1024]{1,0:T(8,128)(2,1)}, u32[]{:S(2)}) copy-start(bf16[128,1024]{1,0:T(8,128)(2,1)} %param.6) | copy-start | bytes 786436
Sparse Core Ops, SparseCore 0:
  34.9 45.3 all-gather.5
  84.4 91.1 all-gather.7
  177.5 93.0 all-gather.9
